TPU v7x, 32 devices: a whole 2x2x4 slice. The times are simulated.
32 devices in a mesh: grp: 4 (over y, core), dev: 8 (over z, x).
Axes of the slice: x: 2, y: 2, z: 4, core: 2. Of those that a mesh axis runs over, the one named last changes fastest.
Arguments:
- targets: float32 [64, 16384], P(None, ('grp', 'dev')), may hold values from -1.7 to 1.7
- source_grid: int32 [64, 4096], P(None, ('grp', 'dev')), may hold values from -1331000 to 1331000
- source_weight: int32 [1, 4096], P(None, ('grp', 'dev')), may hold values from 1 to 1024
Outputs:
- kernel_sum: float32 [16384], P(('grp', 'dev'))
All inputs are finite; a program needn't handle non-finite values.
Results may differ from a plain program's by a relative error of at most 0.00017.
Values sent between devices are 32-bit elements; how exact they have to be, the bound alone decides.
No kernel may reach another device: no remote copies, remote signals or barrier semaphores. Data moves between devices by JAX's collectives and lax.ppermute only.
A program may use at most 64 MiB of HBM per device.

v0:
```python
import functools
import math

import jax
import jax.numpy as jnp
from jax import lax
from jax.experimental import pallas as pl
from jax.experimental.pallas import tpu as pltpu
from jax.sharding import PartitionSpec as P


KERNEL_RATE = 0.7
RATE_LOG2 = KERNEL_RATE * math.log2(math.e)
WEIGHT_ROWS = 8
AXES = ("grp", "dev")
VMEM_LIMIT = 16 * 1024 * 1024
DEAL = (0, 1, 1, 0, 1, 0, 1)


def split(values):
    high = values.astype(jnp.bfloat16)
    return high, (values - high.astype(jnp.float32)).astype(jnp.bfloat16)


def sums_kernel(count_tgt, src_counts, count_add, *refs):
    count_src = len(src_counts)
    tgt_refs, src_refs = refs[:count_tgt], refs[count_tgt : count_tgt + count_src]
    refs = refs[count_tgt + count_src :]
    add_refs, out_refs = refs[:count_add], refs[count_add : count_add + count_tgt]
    tgt_parts, tgt_term = refs[count_add + count_tgt :]
    dim, width = tgt_refs[0].shape
    for i, ref in enumerate(tgt_refs):
        tgt = ref[...]
        cols = pl.ds(i * width, width)
        norm = jnp.sum(tgt * tgt, axis=0, keepdims=True)
        tgt_term[:, cols] = jnp.broadcast_to(-RATE_LOG2 * norm, (8, width))
        high, low = split(tgt * (2.0 * RATE_LOG2))
        tgt_parts[:, cols] = jnp.concatenate([high, low, high, low], axis=0)
    running = [jnp.zeros((8, width), jnp.float32) for _ in range(count_tgt)]
    if count_add:
        running = [ref[...] for ref in add_refs]
    for ref, src_count in zip(src_refs, src_counts):
        points = ref[0:dim, 0:src_count].astype(jnp.float32) * (1.0 / 1048576.0)
        masses = ref[dim : dim + 1, 0:src_count].astype(jnp.float32) * (1.0 / 16.0)
        norm = jnp.sum(points * points, axis=0, keepdims=True)
        term = jnp.log2(masses) - RATE_LOG2 * norm
        term = jnp.broadcast_to(term, (128, src_count)).T
        term = jnp.concatenate([term] * (width // 128), axis=1)
        high, low = split(points)
        src_parts = jnp.concatenate([high, high, low, low], axis=0).T
        for i in range(count_tgt):
            cols = pl.ds(i * width, width)
            inner = jnp.dot(src_parts, tgt_parts[:, cols], preferred_element_type=jnp.float32)
            value = jnp.exp2(inner + tgt_term[0:1, cols] + term)
            running[i] = running[i] + jnp.sum(value.reshape(src_count // 8, 8, width), axis=0)
    for i, ref in enumerate(out_refs):
        if ref.shape[0] == 1:
            ref[...] = jnp.sum(running[i], axis=0, keepdims=True)
        else:
            ref[...] = running[i]


def partial_sums(tgts, srcs, src_counts, adds=(), last=True):
    count_tgt, count_src = len(tgts), len(srcs)
    dim, width = tgts[0].shape
    pairs = count_tgt * width * sum(src_counts)
    in_vmem = pl.BlockSpec(memory_space=pltpu.VMEM)
    return pl.pallas_call(
        functools.partial(sums_kernel, count_tgt, src_counts, len(adds)),
        out_shape=[jax.ShapeDtypeStruct((1 if last else 8, width), jnp.float32)] * count_tgt,
        in_specs=[in_vmem] * (count_tgt + count_src + len(adds)),
        out_specs=[in_vmem] * count_tgt,
        scratch_shapes=[
            pltpu.VMEM((4 * dim, count_tgt * width), jnp.bfloat16),
            pltpu.VMEM((8, count_tgt * width), jnp.float32),
        ],
        compiler_params=pltpu.CompilerParams(vmem_limit_bytes=VMEM_LIMIT),
        cost_estimate=pl.CostEstimate(
            flops=8 * dim * pairs, bytes_accessed=4 * dim * count_tgt * width, transcendentals=pairs
        ),
    )(*tgts, *srcs, *adds)


def moves(groups, devices):
    cores, sides = 2 - groups % 2, 2 - devices % 2
    places = devices // sides
    paired = places & (places - 1) == 0

    def over(change, cores_in=None):
        pairs = []
        for at in range(groups * devices):
            g, d = at // devices, at % devices
            pair, core, place, side = change(g // cores, g % cores, d // sides, d % sides)
            pair, core, place, side = pair % (groups // cores), core % cores, place % places, side % sides
            if cores_in is None or g % cores in cores_in:
                pairs.append((at, (pair * cores + core) * devices + place * sides + side))
        return pairs

    steps = [(p, s) for p in range(places) for s in range(sides) if p or s]
    steps.sort(key=lambda step: (step[0] + step[1], step[0]), reverse=True)
    shares = [[] for _ in range(cores)]
    for i, step in enumerate(steps):
        shares[DEAL[i % len(DEAL)] % cores].append(step)
    shares[0][:2] = shares[0][:2][::-1]
    srcs = []
    for k in range(max(map(len, shares))):
        pairs = []
        for core, share in enumerate(shares):
            if k < len(share):
                far, flip = share[k]
                pairs += over(
                    lambda y, c, p, s, far=far, flip=flip: (y, c, p ^ far if paired else p + far, s + flip), (core,)
                )
        srcs.append(pairs)
    mate = over(lambda y, c, p, s: (y, c + 1, p, s)) if cores == 2 else None
    pairs = [over(lambda y, c, p, s, k=k: (y + k, c, p, s)) for k in range(1, groups // cores)]
    both = [over(lambda y, c, p, s, k=k: (y + k, c + 1, p, s)) for k in range(1, groups // cores)]
    return mate, pairs, both if cores == 2 else [], srcs


def back(move):
    return [(to, at) for at, to in move]


def sent(values, move):
    return lax.ppermute(values, AXES, move)


def placed(part, row, col, size):
    rows, cols = size[0] - row - part.shape[0], size[1] - col - part.shape[1]
    return lax.pad(part, jnp.zeros((), part.dtype), [(row, rows, 0), (col, cols, 0)])


def body(targets, source_grid, source_weight):
    groups, devices = lax.axis_size("grp"), lax.axis_size("dev")
    mate, pairs, both, src_moves = moves(groups, devices)
    dim, count = source_grid.shape
    others = [sent(targets, move) for move in pairs]

    size = (dim + WEIGHT_ROWS, count * (1 if mate is None else 2))
    block = placed(source_grid, 0, 0, size) + placed(source_weight, dim, 0, size)
    if mate is not None:
        block = lax.optimization_barrier(block)
        block = block + placed(sent(source_grid, mate), 0, count, size)
        block = block + placed(sent(source_weight, mate), dim, count, size)
    srcs = [block] + [sent(block, move) for move in src_moves]
    counts = [count] + [src.shape[1] for src in srcs[1:]]

    own = [targets]
    if mate is not None:
        others += [sent(other, mate) for other in others]
        own += [sent(targets, mate)]
    sums = ()
    cuts = sorted({0, min(2, len(srcs) - 1), len(srcs) - 1, len(srcs)})
    for low, high in zip(cuts, cuts[1:]):
        sums = partial_sums(others, srcs[low:high], counts[low:high], sums, high == len(srcs))
    mine = partial_sums(own, srcs, counts)
    total = mine[0]
    for part in mine[1:]:
        total = total + sent(part, mate)
    for part, move in zip(sums, pairs + both):
        total = total + sent(part, back(move))
    return total.reshape(targets.shape[1])


def solution(mesh):
    in_specs = (P(None, ("grp", "dev")), P(None, ("grp", "dev")), P(None, ("grp", "dev")))
    out_specs = P(("grp", "dev"))
    return jax.shard_map(body, mesh=mesh, in_specs=in_specs, out_specs=out_specs, check_vma=False)
```

profile of v0, /device:TPU:1, one launch (start us, length us, event | category | flops | bytes accessed | tf_op | source)
XLA Modules:
  0.0 27.3 jit_solution(3104282322381409522)
XLA Ops:
  0.0 0.0 copy-start
  0.0 0.0 collective-permute-start.2
  0.0 0.5 %collective-permute-start.1 = (s32[64,128]{1,0:T(8,128)}, s32[64,128]{1,0:T(8,128)S(1)}, u32[]{:S(2)}, u32[]{:S(2)}) collective-permute-start(s32[64,128]{1,0:T(8,128)} %param.4), channel_id=1, source_target_pairs={{0,8},{1,9},{2,10},{3,11},{4,12},{5,13},{6,14},{7,15},{8,0},{9,1},... | collective-permute-start | bytes 98312 | tf_op jit(solution)/shard_map/ppermute | solution.py:126
  0.5 2.3 %collective-permute-start.8 = (f32[64,512]{1,0:T(8,128)}, f32[64,512]{1,0:T(8,128)S(1)}, u32[]{:S(2)}, u32[]{:S(2)}) collective-permute-start(f32[64,512]{1,0:T(8,128)} %refs_0_.1), channel_id=1, source_target_pairs={{0,16},{1,17},{2,18},{3,19},{4,20},{5,21},{6,22},{7,23},{8,24},{9,... | collective-permute-start | bytes 393224 | tf_op jit(solution)/shard_map/ppermute | solution.py:126
  2.8 0.8 %pad_add_fusion.1 = s32[72,256]{1,0:T(8,128)S(1)} fusion(s32[1,128]{1,0:T(1,128)} %param.5, s32[64,128]{1,0:T(8,128)} %param.4), kind=kLoop, calls=%fused_computation.1 | loop fusion | flops 18432 | bytes 107008 | tf_op jit(solution)/shard_map/add | solution.py:141
  3.6 0.0 collective-permute-done.2
  3.6 0.0 collective-permute-done.1
  3.6 3.1 %collective-permute-start.6 = (s32[72,256]{1,0:T(8,128)S(1)}, s32[72,256]{1,0:T(8,128)S(1)}, u32[]{:S(2)}, u32[]{:S(2)}) collective-permute-start(s32[72,256]{1,0:T(8,128)S(1)} %pad_add_fusion.refs_2_), channel_id=1, source_target_pairs={{8,9},{9,8},{10,11},{11,10},{12,13},{13,12},{14,15},{15,14},{24,25... | collective-permute-start | bytes 221192 | tf_op jit(solution)/shard_map/ppermute | solution.py:126
  6.7 0.0 copy-done
  6.8 0.1 collective-permute-start
  6.8 0.0 collective-permute-done.8.refs_0_
  6.8 0.6 %collective-permute-start.9 = (f32[64,512]{1,0:T(8,128)S(1)}, f32[64,512]{1,0:T(8,128)S(1)}, u32[]{:S(2)}, u32[]{:S(2)}) collective-permute-start(f32[64,512]{1,0:T(8,128)S(1)} %collective-permute-done.8.refs_0_), channel_id=1, source_target_pairs={{0,8},{1,9},{2,10},{3,11},{4,12},{5,13},{6,14},{7,15},{8,0},{9,1},... | collective-permute-start | bytes 393224 | tf_op jit(solution)/shard_map/ppermute | solution.py:126
  7.5 2.4 %collective-permute-start.5 = (s32[72,256]{1,0:T(8,128)S(1)}, s32[72,256]{1,0:T(8,128)S(1)}, u32[]{:S(2)}, u32[]{:S(2)}) collective-permute-start(s32[72,256]{1,0:T(8,128)S(1)} %pad_add_fusion.refs_2_), channel_id=1, source_target_pairs={{0,2},{1,3},{2,0},{3,1},{4,6},{5,7},{6,4},{7,5},{16,18},{17,19},{1... | collective-permute-start | bytes 221192 | tf_op jit(solution)/shard_map/ppermute | solution.py:126
  9.9 2.3 %collective-permute-start.4 = (s32[72,256]{1,0:T(8,128)S(1)}, s32[72,256]{1,0:T(8,128)S(1)}, u32[]{:S(2)}, u32[]{:S(2)}) collective-permute-start(s32[72,256]{1,0:T(8,128)S(1)} %pad_add_fusion.refs_2_), channel_id=1, source_target_pairs={{0,7},{1,6},{2,5},{3,4},{4,3},{5,2},{6,1},{7,0},{16,23},{17,22},{1... | collective-permute-start | bytes 221192 | tf_op jit(solution)/shard_map/ppermute | solution.py:126
  12.2 0.0 collective-permute-done.6.refs_6_.refs_2_
  12.2 0.0 collective-permute-start.3
  12.2 0.0 collective-permute-done.5.refs_5_.refs_3_
  12.2 6.5 %collective-permute-done.4.refs_4_.refs_2_ = s32[72,256]{1,0:T(8,128)S(1)} collective-permute-done((s32[72,256]{1,0:T(8,128)S(1)}, s32[72,256]{1,0:T(8,128)S(1)}, u32[]{:S(2)}, u32[]{:S(2)}) %collective-permute-start.4) | collective-permute-done | bytes 73760 | tf_op jit(solution)/shard_map/ppermute | solution.py:126
  18.7 0.0 collective-permute-done.3.refs_3_
  18.7 0.0 collective-permute-done.refs_1_
  18.8 1.0 %shard_map.37 = (f32[1,512]{1,0:T(1,128)S(1)}, f32[1,512]{1,0:T(1,128)S(1)}) custom-call(f32[64,512]{1,0:T(8,128)S(1)} %copy-done, f32[64,512]{1,0:T(8,128)S(1)} %collective-permute-done.refs_1_, s32[72,256]{1,0:T(8,128)S(1)} %pad_add_fusion.refs_2_, s32[72,256]{1,0:T(8,128)S(1)} %collective-permute-done.3.refs_3_, ...), custom_call_target="tpu_custom_call" | custom-call | flops 603979776 | bytes 262144 | tf_op jit(solution)/shard_map/pallas_call | solution.py:68
  19.8 1.3 %collective-permute-start.7 = (f32[1,512]{1,0:T(1,128)S(1)}, f32[1,512]{1,0:T(1,128)S(1)}, u32[]{:S(2)}, u32[]{:S(2)}) collective-permute-start(f32[1,512]{1,0:T(1,128)S(1)} %get-tuple-element.14), channel_id=1, source_target_pairs={{0,8},{1,9},{2,10},{3,11},{4,12},{5,13},{6,14},{7,15},{8,0},{9,1},... | collective-permute-start | bytes 6152 | tf_op jit(solution)/shard_map/ppermute | solution.py:126
  21.1 0.0 collective-permute-done.9.refs_1_
  21.1 0.4 %shard_map.38 = (f32[8,512]{1,0:T(8,128)S(1)}, f32[8,512]{1,0:T(8,128)S(1)}) custom-call(f32[64,512]{1,0:T(8,128)S(1)} %collective-permute-done.8.refs_0_, f32[64,512]{1,0:T(8,128)S(1)} %collective-permute-done.9.refs_1_, s32[72,256]{1,0:T(8,128)S(1)} %pad_add_fusion.refs_2_, s32[72,256]{1,0:T(8,128)S(1)} %collective-permute-done.3.refs_3_), custom_call_target="tpu_custom_call" | custom-call | flops 201326592 | bytes 262144 | tf_op jit(solution)/shard_map/pallas_call | solution.py:68
  21.5 0.5 %shard_map.39 = (f32[8,512]{1,0:T(8,128)S(1)}, f32[8,512]{1,0:T(8,128)S(1)}) custom-call(f32[64,512]{1,0:T(8,128)S(1)} %collective-permute-done.8.refs_0_, f32[64,512]{1,0:T(8,128)S(1)} %collective-permute-done.9.refs_1_, s32[72,256]{1,0:T(8,128)S(1)} %collective-permute-done.4.refs_4_.refs_2_, s32[72,256]{1,0:T(8,128)S(1)} %collective-permute-done.5.refs_5_.refs_3_, ...), custom_call_target="tpu_custom_call" | custom-call | flops 268435456 | bytes 262144 | tf_op jit(solution)/shard_map/pallas_call | solution.py:68
  22.0 0.4 %shard_map.40 = (f32[1,512]{1,0:T(1,128)S(1)}, f32[1,512]{1,0:T(1,128)S(1)}) custom-call(f32[64,512]{1,0:T(8,128)S(1)} %collective-permute-done.8.refs_0_, f32[64,512]{1,0:T(8,128)S(1)} %collective-permute-done.9.refs_1_, s32[72,256]{1,0:T(8,128)S(1)} %collective-permute-done.6.refs_6_.refs_2_, f32[8,512]{1,0:T(8,128)S(1)} %get-tuple-element.17.refs_3_, ...), custom_call_target="tpu_custom_call" | custom-call | flops 134217728 | bytes 262144 | tf_op jit(solution)/shard_map/pallas_call | solution.py:68
  22.4 1.3 %collective-permute-start.10 = (f32[1,512]{1,0:T(1,128)S(1)}, f32[1,512]{1,0:T(1,128)S(1)}, u32[]{:S(2)}, u32[]{:S(2)}) collective-permute-start(f32[1,512]{1,0:T(1,128)S(1)} %get-tuple-element.19), channel_id=1, source_target_pairs={{16,0},{17,1},{18,2},{19,3},{20,4},{21,5},{22,6},{23,7},{24,8},{25... | collective-permute-start | bytes 6152 | tf_op jit(solution)/shard_map/ppermute | solution.py:126
  23.7 0.4 %collective-permute-start.11 = (f32[1,512]{1,0:T(1,128)S(1)}, f32[1,512]{1,0:T(1,128)S(1)}, u32[]{:S(2)}, u32[]{:S(2)}) collective-permute-start(f32[1,512]{1,0:T(1,128)S(1)} %get-tuple-element.20), channel_id=1, source_target_pairs={{24,0},{25,1},{26,2},{27,3},{28,4},{29,5},{30,6},{31,7},{16,8},{17... | collective-permute-start | bytes 6152 | tf_op jit(solution)/shard_map/ppermute | solution.py:126
  24.1 0.0 collective-permute-done.7
  24.1 0.8 %collective-permute-done.10 = f32[1,512]{1,0:T(1,128)S(1)} collective-permute-done((f32[1,512]{1,0:T(1,128)S(1)}, f32[1,512]{1,0:T(1,128)S(1)}, u32[]{:S(2)}, u32[]{:S(2)}) %collective-permute-start.10) | collective-permute-done | bytes 2080 | tf_op jit(solution)/shard_map/ppermute | solution.py:126
  24.9 1.8 %collective-permute-done.11 = f32[1,512]{1,0:T(1,128)S(1)} collective-permute-done((f32[1,512]{1,0:T(1,128)S(1)}, f32[1,512]{1,0:T(1,128)S(1)}, u32[]{:S(2)}, u32[]{:S(2)}) %collective-permute-start.11) | collective-permute-done | bytes 2080 | tf_op jit(solution)/shard_map/ppermute | solution.py:126
  26.7 0.6 %add_add_fusion = f32[1,512]{1,0:T(1,128)} fusion(f32[1,512]{1,0:T(1,128)S(1)} %collective-permute-done.11, f32[1,512]{1,0:T(1,128)S(1)} %collective-permute-done.10, f32[1,512]{1,0:T(1,128)S(1)} %get-tuple-element.13, f32[1,512]{1,0:T(1,128)S(1)} %collective-permute-done.7), kind=kLoop, calls=%fused_computation.2 | loop fusion | flops 1536 | bytes 10240 | tf_op jit(solution)/shard_map/add | solution.py:162
  (1 shorter events, 0.0 us)
Async XLA Ops:
  0.0 6.7 %copy-start = (f32[64,512]{1,0:T(8,128)S(1)}, f32[64,512]{1,0:T(8,128)}, u32[]{:S(2)}) copy-start(f32[64,512]{1,0:T(8,128)} %refs_0_.1) | copy-start | bytes 393220
  0.0 3.6 %collective-permute-start.2 = (s32[1,128]{1,0:T(1,128)}, s32[1,128]{1,0:T(1,128)S(1)}, u32[]{:S(2)}, u32[]{:S(2)}) collective-permute-start(s32[1,128]{1,0:T(1,128)} %param.5), channel_id=1, source_target_pairs={{0,8},{1,9},{2,10},{3,11},{4,12},{5,13},{6,14},{7,15},{8,0},{9,1},... | collective-permute-start | bytes 1544 | tf_op jit(solution)/shard_map/ppermute | solution.py:126
  0.0 3.6 %collective-permute-start.1 = (s32[64,128]{1,0:T(8,128)}, s32[64,128]{1,0:T(8,128)S(1)}, u32[]{:S(2)}, u32[]{:S(2)}) collective-permute-start(s32[64,128]{1,0:T(8,128)} %param.4), channel_id=1, source_target_pairs={{0,8},{1,9},{2,10},{3,11},{4,12},{5,13},{6,14},{7,15},{8,0},{9,1},... | collective-permute-start | bytes 98312 | tf_op jit(solution)/shard_map/ppermute | solution.py:126
  0.5 6.3 %collective-permute-start.8 = (f32[64,512]{1,0:T(8,128)}, f32[64,512]{1,0:T(8,128)S(1)}, u32[]{:S(2)}, u32[]{:S(2)}) collective-permute-start(f32[64,512]{1,0:T(8,128)} %refs_0_.1), channel_id=1, source_target_pairs={{0,16},{1,17},{2,18},{3,19},{4,20},{5,21},{6,22},{7,23},{8,24},{9,... | collective-permute-start | bytes 393224 | tf_op jit(solution)/shard_map/ppermute | solution.py:126
  3.6 8.6 %collective-permute-start.6 = (s32[72,256]{1,0:T(8,128)S(1)}, s32[72,256]{1,0:T(8,128)S(1)}, u32[]{:S(2)}, u32[]{:S(2)}) collective-permute-start(s32[72,256]{1,0:T(8,128)S(1)} %pad_add_fusion.refs_2_), channel_id=1, source_target_pairs={{8,9},{9,8},{10,11},{11,10},{12,13},{13,12},{14,15},{15,14},{24,25... | collective-permute-start | bytes 221192 | tf_op jit(solution)/shard_map/ppermute | solution.py:126
  6.8 12.0 %collective-permute-start = (f32[64,512]{1,0:T(8,128)S(1)}, f32[64,512]{1,0:T(8,128)S(1)}, u32[]{:S(2)}, u32[]{:S(2)}) collective-permute-start(f32[64,512]{1,0:T(8,128)S(1)} %copy-done), channel_id=1, source_target_pairs={{0,8},{1,9},{2,10},{3,11},{4,12},{5,13},{6,14},{7,15},{8,0},{9,1},... | collective-permute-start | bytes 393224 | tf_op jit(solution)/shard_map/ppermute | solution.py:126
  6.8 14.2 %collective-permute-start.9 = (f32[64,512]{1,0:T(8,128)S(1)}, f32[64,512]{1,0:T(8,128)S(1)}, u32[]{:S(2)}, u32[]{:S(2)}) collective-permute-start(f32[64,512]{1,0:T(8,128)S(1)} %collective-permute-done.8.refs_0_), channel_id=1, source_target_pairs={{0,8},{1,9},{2,10},{3,11},{4,12},{5,13},{6,14},{7,15},{8,0},{9,1},... | collective-permute-start | bytes 393224 | tf_op jit(solution)/shard_map/ppermute | solution.py:126
  7.5 4.7 %collective-permute-start.5 = (s32[72,256]{1,0:T(8,128)S(1)}, s32[72,256]{1,0:T(8,128)S(1)}, u32[]{:S(2)}, u32[]{:S(2)}) collective-permute-start(s32[72,256]{1,0:T(8,128)S(1)} %pad_add_fusion.refs_2_), channel_id=1, source_target_pairs={{0,2},{1,3},{2,0},{3,1},{4,6},{5,7},{6,4},{7,5},{16,18},{17,19},{1... | collective-permute-start | bytes 221192 | tf_op jit(solution)/shard_map/ppermute | solution.py:126
  9.9 8.8 %collective-permute-start.4 = (s32[72,256]{1,0:T(8,128)S(1)}, s32[72,256]{1,0:T(8,128)S(1)}, u32[]{:S(2)}, u32[]{:S(2)}) collective-permute-start(s32[72,256]{1,0:T(8,128)S(1)} %pad_add_fusion.refs_2_), channel_id=1, source_target_pairs={{0,7},{1,6},{2,5},{3,4},{4,3},{5,2},{6,1},{7,0},{16,23},{17,22},{1... | collective-permute-start | bytes 221192 | tf_op jit(solution)/shard_map/ppermute | solution.py:126
  12.2 6.6 %collective-permute-start.3 = (s32[72,256]{1,0:T(8,128)S(1)}, s32[72,256]{1,0:T(8,128)S(1)}, u32[]{:S(2)}, u32[]{:S(2)}) collective-permute-start(s32[72,256]{1,0:T(8,128)S(1)} %pad_add_fusion.refs_2_), channel_id=1, source_target_pairs={{0,4},{1,5},{2,6},{3,7},{4,0},{5,1},{6,2},{7,3},{16,20},{17,21},{1... | collective-permute-start | bytes 221192 | tf_op jit(solution)/shard_map/ppermute | solution.py:126
  19.8 4.3 %collective-permute-start.7 = (f32[1,512]{1,0:T(1,128)S(1)}, f32[1,512]{1,0:T(1,128)S(1)}, u32[]{:S(2)}, u32[]{:S(2)}) collective-permute-start(f32[1,512]{1,0:T(1,128)S(1)} %get-tuple-element.14), channel_id=1, source_target_pairs={{0,8},{1,9},{2,10},{3,11},{4,12},{5,13},{6,14},{7,15},{8,0},{9,1},... | collective-permute-start | bytes 6152 | tf_op jit(solution)/shard_map/ppermute | solution.py:126
  22.4 2.5 %collective-permute-start.10 = (f32[1,512]{1,0:T(1,128)S(1)}, f32[1,512]{1,0:T(1,128)S(1)}, u32[]{:S(2)}, u32[]{:S(2)}) collective-permute-start(f32[1,512]{1,0:T(1,128)S(1)} %get-tuple-element.19), channel_id=1, source_target_pairs={{16,0},{17,1},{18,2},{19,3},{20,4},{21,5},{22,6},{23,7},{24,8},{25... | collective-permute-start | bytes 6152 | tf_op jit(solution)/shard_map/ppermute | solution.py:126
  23.7 3.0 %collective-permute-start.11 = (f32[1,512]{1,0:T(1,128)S(1)}, f32[1,512]{1,0:T(1,128)S(1)}, u32[]{:S(2)}, u32[]{:S(2)}) collective-permute-start(f32[1,512]{1,0:T(1,128)S(1)} %get-tuple-element.20), channel_id=1, source_target_pairs={{24,0},{25,1},{26,2},{27,3},{28,4},{29,5},{30,6},{31,7},{16,8},{17... | collective-permute-start | bytes 6152 | tf_op jit(solution)/shard_map/ppermute | solution.py:126
where the time goes:
time: 27.8 us; the launch traced here: 27.3 us
  starting transfers between devices  14.3 us (51%)
  waiting for transfers between devices  9.16 us (33%)
  Pallas kernels  2.34 us (8%)
  other arithmetic  1.37 us (5%)
    ppermute x12, starting transfers between devices, sent(): return lax.ppermute(values, AXES, move)  14.3 us
    ppermute x12, waiting for transfers between devices, sent(): return lax.ppermute(values, AXES, move)  9.16 us
    pallas_call x4, Pallas kernels, partial_sums(): pl.pallas_call(functools.partial(sums_kernel, count_tgt, src_counts, len(...  2.34 us
    add x1, other arithmetic, body(): placed(source_grid, 0, 0, size) + placed(source_weight, dim, 0, size)  0.78 us
    add x1, other arithmetic, body(): total = total + sent(part, back(move))  0.58 us
  transfers between devices with their start and end apart: 12, of which 3 were waited for; matrix products, arithmetic and copies ran while one was open for 3% of the time, Pallas kernels for 9%

commit v1 on v0

--- a/solution.py
+++ b/solution.py
@@ -99,6 +99,7 @@
     steps = [(p, s) for p in range(places) for s in range(sides) if p or s]
     steps.sort(key=lambda step: (step[0] + step[1], step[0]), reverse=True)
     shares = [[] for _ in range(cores)]
+    half = [steps.pop()] if cores == 2 and steps else []
     for i, step in enumerate(steps):
         shares[DEAL[i % len(DEAL)] % cores].append(step)
     shares[0][:2] = shares[0][:2][::-1]
@@ -112,6 +113,8 @@
                     lambda y, c, p, s, far=far, flip=flip: (y, c, p ^ far if paired else p + far, s + flip), (core,)
                 )
         srcs.append(pairs)
+    for far, flip in half:
+        srcs.append(over(lambda y, c, p, s: (y, c, p ^ far if paired else p + far, s + flip)))
     mate = over(lambda y, c, p, s: (y, c + 1, p, s)) if cores == 2 else None
     pairs = [over(lambda y, c, p, s, k=k: (y + k, c, p, s)) for k in range(1, groups // cores)]
     both = [over(lambda y, c, p, s, k=k: (y + k, c + 1, p, s)) for k in range(1, groups // cores)]
@@ -143,7 +146,10 @@
         block = lax.optimization_barrier(block)
         block = block + placed(sent(source_grid, mate), 0, count, size)
         block = block + placed(sent(source_weight, mate), dim, count, size)
-    srcs = [block] + [sent(block, move) for move in src_moves]
+    single = block if mate is None else block[:, :count]
+    srcs = [block]
+    for i, move in enumerate(src_moves):
+        srcs.append(sent(single if i == len(src_moves) - 1 else block, move))
     counts = [count] + [src.shape[1] for src in srcs[1:]]
 
     own = [targets]
@@ -151,9 +157,13 @@
         others += [sent(other, mate) for other in others]
         own += [sent(targets, mate)]
     sums = ()
-    cuts = sorted({0, min(2, len(srcs) - 1), len(srcs) - 1, len(srcs)})
-    for low, high in zip(cuts, cuts[1:]):
-        sums = partial_sums(others, srcs[low:high], counts[low:high], sums, high == len(srcs))
+    index = list(range(len(srcs)))
+    late = sorted({index[-1], min(2, index[-1])})
+    early = [i for i in index[:2] if i not in late]
+    groups_of = [part for part in (early, [i for i in index if i not in early + late], late) if part]
+    for i, part in enumerate(groups_of):
+        is_last = i == len(groups_of) - 1
+        sums = partial_sums(others, [srcs[k] for k in part], [counts[k] for k in part], sums, is_last)
     mine = partial_sums(own, srcs, counts)
     total = mine[0]
     for part in mine[1:]:

time: 27.8 us -> 27.5 us (0.989)
  starting transfers between devices: 14.3 us -> 12.8 us
  waiting for transfers between devices: 9.16 us -> 10.6 us
    ppermute x12, starting transfers between devices: 14.3 us -> 12.8 us  [sent(): return lax.ppermute(values, AXES, move)]
    ppermute x12, waiting for transfers between devices: 9.16 us -> 10.6 us  [sent(): return lax.ppermute(values, AXES, move)]
  transfers between devices with their start and end apart: 12 -> 12, of which waited for: 3 -> 5; matrix products, arithmetic and copies ran while one was open for 3% -> 3% of each run, Pallas kernels for 9% -> 8%
where the time goes in v1:
time: 27.5 us; the launch traced here: 27.1 us
  starting transfers between devices  12.8 us (47%)
  waiting for transfers between devices  10.6 us (39%)
  Pallas kernels  2.19 us (8%)
  other arithmetic  1.37 us (5%)
    ppermute x12, starting transfers between devices, sent(): return lax.ppermute(values, AXES, move)  12.8 us
    ppermute x12, waiting for transfers between devices, sent(): return lax.ppermute(values, AXES, move)  10.6 us
    pallas_call x4, Pallas kernels, partial_sums(): pl.pallas_call(functools.partial(sums_kernel, count_tgt, src_counts, len(...  2.19 us
    add x1, other arithmetic, body(): placed(source_grid, 0, 0, size) + placed(source_weight, dim, 0, size)  0.78 us
    add x1, other arithmetic, body(): total = total + sent(part, back(move))  0.58 us
  transfers between devices with their start and end apart: 12, of which 5 were waited for; matrix products, arithmetic and copies ran while one was open for 3% of the time, Pallas kernels for 8%

profile of v1, /device:TPU:1, one launch (start us, length us, event | category | flops | bytes accessed | tf_op | source)
XLA Modules:
  0.0 27.1 jit_solution(18284498589838039848)
XLA Ops:
  0.0 0.0 collective-permute-start
  0.0 2.7 %collective-permute-start.8 = (f32[64,512]{1,0:T(8,128)}, f32[64,512]{1,0:T(8,128)S(1)}, u32[]{:S(2)}, u32[]{:S(2)}) collective-permute-start(f32[64,512]{1,0:T(8,128)} %refs_0_.1), channel_id=1, source_target_pairs={{0,16},{1,17},{2,18},{3,19},{4,20},{5,21},{6,22},{7,23},{8,24},{9,... | collective-permute-start | bytes 393224 | tf_op jit(solution)/shard_map/ppermute | solution.py:129
  2.7 0.3 %collective-permute-start.2 = (s32[1,128]{1,0:T(1,128)}, s32[1,128]{1,0:T(1,128)S(1)}, u32[]{:S(2)}, u32[]{:S(2)}) collective-permute-start(s32[1,128]{1,0:T(1,128)} %param.5), channel_id=1, source_target_pairs={{0,8},{1,9},{2,10},{3,11},{4,12},{5,13},{6,14},{7,15},{8,0},{9,1},... | collective-permute-start | bytes 1544 | tf_op jit(solution)/shard_map/ppermute | solution.py:129
  3.0 0.2 collective-permute-start.1
  3.2 0.8 %pad_add_fusion.1 = s32[72,256]{1,0:T(8,128)S(1)} fusion(s32[1,128]{1,0:T(1,128)} %param.5, s32[64,128]{1,0:T(8,128)} %param.4), kind=kLoop, calls=%fused_computation.1 | loop fusion | flops 18432 | bytes 107008 | tf_op jit(solution)/shard_map/add | solution.py:144
  4.0 0.0 copy-start
  4.0 0.0 collective-permute-done.2
  4.0 0.4 %collective-permute-done.1 = s32[64,128]{1,0:T(8,128)S(1)} collective-permute-done((s32[64,128]{1,0:T(8,128)}, s32[64,128]{1,0:T(8,128)S(1)}, u32[]{:S(2)}, u32[]{:S(2)}) %collective-permute-start.1) | collective-permute-done | bytes 32800 | tf_op jit(solution)/shard_map/ppermute | solution.py:129
  4.5 1.3 %collective-permute-start.6 = (s32[72,128]{1,0:T(8,128)S(1)}, s32[72,128]{1,0:T(8,128)S(1)}, u32[]{:S(2)}, u32[]{:S(2)}) collective-permute-start(s32[72,128]{1,0:T(8,128)S(1)} %slice.4), channel_id=1, source_target_pairs={{0,1},{1,0},{2,3},{3,2},{4,5},{5,4},{6,7},{7,6},{8,9},{9,8},{10,11... | collective-permute-start | bytes 110600 | tf_op jit(solution)/shard_map/ppermute | solution.py:129
  5.7 1.1 %collective-permute-done.8.refs_0_ = f32[64,512]{1,0:T(8,128)S(1)} collective-permute-done((f32[64,512]{1,0:T(8,128)}, f32[64,512]{1,0:T(8,128)S(1)}, u32[]{:S(2)}, u32[]{:S(2)}) %collective-permute-start.8) | collective-permute-done | bytes 131104 | tf_op jit(solution)/shard_map/ppermute | solution.py:129
  6.8 0.6 %collective-permute-start.9 = (f32[64,512]{1,0:T(8,128)S(1)}, f32[64,512]{1,0:T(8,128)S(1)}, u32[]{:S(2)}, u32[]{:S(2)}) collective-permute-start(f32[64,512]{1,0:T(8,128)S(1)} %collective-permute-done.8.refs_0_), channel_id=1, source_target_pairs={{0,8},{1,9},{2,10},{3,11},{4,12},{5,13},{6,14},{7,15},{8,0},{9,1},... | collective-permute-start | bytes 393224 | tf_op jit(solution)/shard_map/ppermute | solution.py:129
  7.4 2.4 %collective-permute-start.5 = (s32[72,256]{1,0:T(8,128)S(1)}, s32[72,256]{1,0:T(8,128)S(1)}, u32[]{:S(2)}, u32[]{:S(2)}) collective-permute-start(s32[72,256]{1,0:T(8,128)S(1)} %pad_add_fusion.refs_2_), channel_id=1, source_target_pairs={{0,2},{1,3},{2,0},{3,1},{4,6},{5,7},{6,4},{7,5},{16,18},{17,19},{1... | collective-permute-start | bytes 221192 | tf_op jit(solution)/shard_map/ppermute | solution.py:129
  9.8 2.3 %collective-permute-start.4 = (s32[72,256]{1,0:T(8,128)S(1)}, s32[72,256]{1,0:T(8,128)S(1)}, u32[]{:S(2)}, u32[]{:S(2)}) collective-permute-start(s32[72,256]{1,0:T(8,128)S(1)} %pad_add_fusion.refs_2_), channel_id=1, source_target_pairs={{0,7},{1,6},{2,5},{3,4},{4,3},{5,2},{6,1},{7,0},{16,23},{17,22},{1... | collective-permute-start | bytes 221192 | tf_op jit(solution)/shard_map/ppermute | solution.py:129
  12.1 0.0 collective-permute-done.6.refs_6_.refs_3_
  12.1 0.0 collective-permute-start.3
  12.1 0.0 collective-permute-done.5.refs_5_.refs_2_
  12.1 6.5 %collective-permute-done.4.refs_4_.refs_2_ = s32[72,256]{1,0:T(8,128)S(1)} collective-permute-done((s32[72,256]{1,0:T(8,128)S(1)}, s32[72,256]{1,0:T(8,128)S(1)}, u32[]{:S(2)}, u32[]{:S(2)}) %collective-permute-start.4) | collective-permute-done | bytes 73760 | tf_op jit(solution)/shard_map/ppermute | solution.py:129
  18.7 0.0 collective-permute-done.3.refs_3_
  18.7 0.0 collective-permute-done.refs_1_
  18.7 0.0 copy-done
  18.7 1.0 %shard_map.37 = (f32[1,512]{1,0:T(1,128)S(1)}, f32[1,512]{1,0:T(1,128)S(1)}) custom-call(f32[64,512]{1,0:T(8,128)S(1)} %copy-done, f32[64,512]{1,0:T(8,128)S(1)} %collective-permute-done.refs_1_, s32[72,256]{1,0:T(8,128)S(1)} %pad_add_fusion.refs_2_, s32[72,256]{1,0:T(8,128)S(1)} %collective-permute-done.3.refs_3_, ...), custom_call_target="tpu_custom_call" | custom-call | flops 536870912 | bytes 262144 | tf_op jit(solution)/shard_map/pallas_call | solution.py:68
  19.7 1.3 %collective-permute-start.7 = (f32[1,512]{1,0:T(1,128)S(1)}, f32[1,512]{1,0:T(1,128)S(1)}, u32[]{:S(2)}, u32[]{:S(2)}) collective-permute-start(f32[1,512]{1,0:T(1,128)S(1)} %get-tuple-element.14), channel_id=1, source_target_pairs={{0,8},{1,9},{2,10},{3,11},{4,12},{5,13},{6,14},{7,15},{8,0},{9,1},... | collective-permute-start | bytes 6152 | tf_op jit(solution)/shard_map/ppermute | solution.py:129
  20.9 0.0 collective-permute-done.9.refs_1_
  20.9 0.4 %shard_map.38 = (f32[8,512]{1,0:T(8,128)S(1)}, f32[8,512]{1,0:T(8,128)S(1)}) custom-call(f32[64,512]{1,0:T(8,128)S(1)} %collective-permute-done.8.refs_0_, f32[64,512]{1,0:T(8,128)S(1)} %collective-permute-done.9.refs_1_, s32[72,256]{1,0:T(8,128)S(1)} %pad_add_fusion.refs_2_, s32[72,256]{1,0:T(8,128)S(1)} %collective-permute-done.3.refs_3_), custom_call_target="tpu_custom_call" | custom-call | flops 201326592 | bytes 262144 | tf_op jit(solution)/shard_map/pallas_call | solution.py:68
  21.4 0.3 %shard_map.39 = (f32[8,512]{1,0:T(8,128)S(1)}, f32[8,512]{1,0:T(8,128)S(1)}) custom-call(f32[64,512]{1,0:T(8,128)S(1)} %collective-permute-done.8.refs_0_, f32[64,512]{1,0:T(8,128)S(1)} %collective-permute-done.9.refs_1_, s32[72,256]{1,0:T(8,128)S(1)} %collective-permute-done.5.refs_5_.refs_2_, f32[8,512]{1,0:T(8,128)S(1)} %get-tuple-element.15.refs_3_, ...), custom_call_target="tpu_custom_call" | custom-call | flops 134217728 | bytes 262144 | tf_op jit(solution)/shard_map/pallas_call | solution.py:68
  21.7 0.5 %shard_map.40 = (f32[1,512]{1,0:T(1,128)S(1)}, f32[1,512]{1,0:T(1,128)S(1)}) custom-call(f32[64,512]{1,0:T(8,128)S(1)} %collective-permute-done.8.refs_0_, f32[64,512]{1,0:T(8,128)S(1)} %collective-permute-done.9.refs_1_, s32[72,256]{1,0:T(8,128)S(1)} %collective-permute-done.4.refs_4_.refs_2_, s32[72,128]{1,0:T(8,128)S(1)} %collective-permute-done.6.refs_6_.refs_3_, ...), custom_call_target="tpu_custom_call" | custom-call | flops 201326592 | bytes 262144 | tf_op jit(solution)/shard_map/pallas_call | solution.py:68
  22.2 1.3 %collective-permute-start.10 = (f32[1,512]{1,0:T(1,128)S(1)}, f32[1,512]{1,0:T(1,128)S(1)}, u32[]{:S(2)}, u32[]{:S(2)}) collective-permute-start(f32[1,512]{1,0:T(1,128)S(1)} %get-tuple-element.19), channel_id=1, source_target_pairs={{16,0},{17,1},{18,2},{19,3},{20,4},{21,5},{22,6},{23,7},{24,8},{25... | collective-permute-start | bytes 6152 | tf_op jit(solution)/shard_map/ppermute | solution.py:129
  23.5 0.4 %collective-permute-start.11 = (f32[1,512]{1,0:T(1,128)S(1)}, f32[1,512]{1,0:T(1,128)S(1)}, u32[]{:S(2)}, u32[]{:S(2)}) collective-permute-start(f32[1,512]{1,0:T(1,128)S(1)} %get-tuple-element.20), channel_id=1, source_target_pairs={{24,0},{25,1},{26,2},{27,3},{28,4},{29,5},{30,6},{31,7},{16,8},{17... | collective-permute-start | bytes 6152 | tf_op jit(solution)/shard_map/ppermute | solution.py:129
  23.9 0.0 collective-permute-done.7
  23.9 0.8 %collective-permute-done.10 = f32[1,512]{1,0:T(1,128)S(1)} collective-permute-done((f32[1,512]{1,0:T(1,128)S(1)}, f32[1,512]{1,0:T(1,128)S(1)}, u32[]{:S(2)}, u32[]{:S(2)}) %collective-permute-start.10) | collective-permute-done | bytes 2080 | tf_op jit(solution)/shard_map/ppermute | solution.py:129
  24.7 1.8 %collective-permute-done.11 = f32[1,512]{1,0:T(1,128)S(1)} collective-permute-done((f32[1,512]{1,0:T(1,128)S(1)}, f32[1,512]{1,0:T(1,128)S(1)}, u32[]{:S(2)}, u32[]{:S(2)}) %collective-permute-start.11) | collective-permute-done | bytes 2080 | tf_op jit(solution)/shard_map/ppermute | solution.py:129
  26.5 0.6 %add_add_fusion = f32[1,512]{1,0:T(1,128)} fusion(f32[1,512]{1,0:T(1,128)S(1)} %collective-permute-done.11, f32[1,512]{1,0:T(1,128)S(1)} %collective-permute-done.10, f32[1,512]{1,0:T(1,128)S(1)} %get-tuple-element.13, f32[1,512]{1,0:T(1,128)S(1)} %collective-permute-done.7), kind=kLoop, calls=%fused_computation.2 | loop fusion | flops 1536 | bytes 10240 | tf_op jit(solution)/shard_map/add | solution.py:172
  (2 shorter events, 0.0 us)
Async XLA Ops:
  0.0 18.7 %collective-permute-start = (f32[64,512]{1,0:T(8,128)}, f32[64,512]{1,0:T(8,128)S(1)}, u32[]{:S(2)}, u32[]{:S(2)}) collective-permute-start(f32[64,512]{1,0:T(8,128)} %refs_0_.1), channel_id=1, source_target_pairs={{0,8},{1,9},{2,10},{3,11},{4,12},{5,13},{6,14},{7,15},{8,0},{9,1},... | collective-permute-start | bytes 393224 | tf_op jit(solution)/shard_map/ppermute | solution.py:129
  0.0 6.8 %collective-permute-start.8 = (f32[64,512]{1,0:T(8,128)}, f32[64,512]{1,0:T(8,128)S(1)}, u32[]{:S(2)}, u32[]{:S(2)}) collective-permute-start(f32[64,512]{1,0:T(8,128)} %refs_0_.1), channel_id=1, source_target_pairs={{0,16},{1,17},{2,18},{3,19},{4,20},{5,21},{6,22},{7,23},{8,24},{9,... | collective-permute-start | bytes 393224 | tf_op jit(solution)/shard_map/ppermute | solution.py:129
  2.7 1.3 %collective-permute-start.2 = (s32[1,128]{1,0:T(1,128)}, s32[1,128]{1,0:T(1,128)S(1)}, u32[]{:S(2)}, u32[]{:S(2)}) collective-permute-start(s32[1,128]{1,0:T(1,128)} %param.5), channel_id=1, source_target_pairs={{0,8},{1,9},{2,10},{3,11},{4,12},{5,13},{6,14},{7,15},{8,0},{9,1},... | collective-permute-start | bytes 1544 | tf_op jit(solution)/shard_map/ppermute | solution.py:129
  3.0 1.4 %collective-permute-start.1 = (s32[64,128]{1,0:T(8,128)}, s32[64,128]{1,0:T(8,128)S(1)}, u32[]{:S(2)}, u32[]{:S(2)}) collective-permute-start(s32[64,128]{1,0:T(8,128)} %param.4), channel_id=1, source_target_pairs={{0,8},{1,9},{2,10},{3,11},{4,12},{5,13},{6,14},{7,15},{8,0},{9,1},... | collective-permute-start | bytes 98312 | tf_op jit(solution)/shard_map/ppermute | solution.py:129
  4.0 14.7 %copy-start = (f32[64,512]{1,0:T(8,128)S(1)}, f32[64,512]{1,0:T(8,128)}, u32[]{:S(2)}) copy-start(f32[64,512]{1,0:T(8,128)} %refs_0_.1) | copy-start | bytes 393220
  4.5 7.7 %collective-permute-start.6 = (s32[72,128]{1,0:T(8,128)S(1)}, s32[72,128]{1,0:T(8,128)S(1)}, u32[]{:S(2)}, u32[]{:S(2)}) collective-permute-start(s32[72,128]{1,0:T(8,128)S(1)} %slice.4), channel_id=1, source_target_pairs={{0,1},{1,0},{2,3},{3,2},{4,5},{5,4},{6,7},{7,6},{8,9},{9,8},{10,11... | collective-permute-start | bytes 110600 | tf_op jit(solution)/shard_map/ppermute | solution.py:129
  6.8 14.1 %collective-permute-start.9 = (f32[64,512]{1,0:T(8,128)S(1)}, f32[64,512]{1,0:T(8,128)S(1)}, u32[]{:S(2)}, u32[]{:S(2)}) collective-permute-start(f32[64,512]{1,0:T(8,128)S(1)} %collective-permute-done.8.refs_0_), channel_id=1, source_target_pairs={{0,8},{1,9},{2,10},{3,11},{4,12},{5,13},{6,14},{7,15},{8,0},{9,1},... | collective-permute-start | bytes 393224 | tf_op jit(solution)/shard_map/ppermute | solution.py:129
  7.4 4.7 %collective-permute-start.5 = (s32[72,256]{1,0:T(8,128)S(1)}, s32[72,256]{1,0:T(8,128)S(1)}, u32[]{:S(2)}, u32[]{:S(2)}) collective-permute-start(s32[72,256]{1,0:T(8,128)S(1)} %pad_add_fusion.refs_2_), channel_id=1, source_target_pairs={{0,2},{1,3},{2,0},{3,1},{4,6},{5,7},{6,4},{7,5},{16,18},{17,19},{1... | collective-permute-start | bytes 221192 | tf_op jit(solution)/shard_map/ppermute | solution.py:129
  9.8 8.8 %collective-permute-start.4 = (s32[72,256]{1,0:T(8,128)S(1)}, s32[72,256]{1,0:T(8,128)S(1)}, u32[]{:S(2)}, u32[]{:S(2)}) collective-permute-start(s32[72,256]{1,0:T(8,128)S(1)} %pad_add_fusion.refs_2_), channel_id=1, source_target_pairs={{0,7},{1,6},{2,5},{3,4},{4,3},{5,2},{6,1},{7,0},{16,23},{17,22},{1... | collective-permute-start | bytes 221192 | tf_op jit(solution)/shard_map/ppermute | solution.py:129
  12.1 6.6 %collective-permute-start.3 = (s32[72,256]{1,0:T(8,128)S(1)}, s32[72,256]{1,0:T(8,128)S(1)}, u32[]{:S(2)}, u32[]{:S(2)}) collective-permute-start(s32[72,256]{1,0:T(8,128)S(1)} %pad_add_fusion.refs_2_), channel_id=1, source_target_pairs={{0,4},{1,5},{2,6},{3,7},{4,0},{5,1},{6,2},{7,3},{16,20},{17,21},{1... | collective-permute-start | bytes 221192 | tf_op jit(solution)/shard_map/ppermute | solution.py:129
  19.7 4.2 %collective-permute-start.7 = (f32[1,512]{1,0:T(1,128)S(1)}, f32[1,512]{1,0:T(1,128)S(1)}, u32[]{:S(2)}, u32[]{:S(2)}) collective-permute-start(f32[1,512]{1,0:T(1,128)S(1)} %get-tuple-element.14), channel_id=1, source_target_pairs={{0,8},{1,9},{2,10},{3,11},{4,12},{5,13},{6,14},{7,15},{8,0},{9,1},... | collective-permute-start | bytes 6152 | tf_op jit(solution)/shard_map/ppermute | solution.py:129
  22.2 2.5 %collective-permute-start.10 = (f32[1,512]{1,0:T(1,128)S(1)}, f32[1,512]{1,0:T(1,128)S(1)}, u32[]{:S(2)}, u32[]{:S(2)}) collective-permute-start(f32[1,512]{1,0:T(1,128)S(1)} %get-tuple-element.19), channel_id=1, source_target_pairs={{16,0},{17,1},{18,2},{19,3},{20,4},{21,5},{22,6},{23,7},{24,8},{25... | collective-permute-start | bytes 6152 | tf_op jit(solution)/shard_map/ppermute | solution.py:129
  23.5 3.0 %collective-permute-start.11 = (f32[1,512]{1,0:T(1,128)S(1)}, f32[1,512]{1,0:T(1,128)S(1)}, u32[]{:S(2)}, u32[]{:S(2)}) collective-permute-start(f32[1,512]{1,0:T(1,128)S(1)} %get-tuple-element.20), channel_id=1, source_target_pairs={{24,0},{25,1},{26,2},{27,3},{28,4},{29,5},{30,6},{31,7},{16,8},{17... | collective-permute-start | bytes 6152 | tf_op jit(solution)/shard_map/ppermute | solution.py:129
